TPU v7x, 32 devices: a whole 2x2x4 slice. The times are simulated.
32 devices in a mesh: groups: 2 (over x), ep: 8 (over z, y), tp: 2 (over core).
Axes of the slice: x: 2, y: 2, z: 4, core: 2. Of those that a mesh axis runs over, the one named last changes fastest.
Arguments:
- hidden: bfloat16 [256, 3584], P(('groups', 'ep'), 'tp'), parts along dimension 0, may hold values from -6 to 6
- routes: int32 [256, 4], P(('groups', 'ep')), parts along dimension 0, may hold values from 0 to 7, as said below
- router_weight: bfloat16 [3584, 8], P('tp'), may hold values from -0.1875 to 0.1875
- gate_weight: bfloat16 [8, 3584, 1024], P('ep', None, 'tp'), may hold values from -0.09375 to 0.09375
- up_weight: bfloat16 [8, 3584, 1024], P('ep', None, 'tp'), may hold values from -0.09375 to 0.09375
- down_weight: bfloat16 [8, 1024, 3584], P('ep', 'tp'), may hold values from -0.1875 to 0.1875
- q_latent: bfloat16 [64, 64, 512], P(('groups', 'ep'), 'tp'), parts along dimension 0, may hold values from -48 to 48
- q_rope: bfloat16 [64, 64, 64], P(('groups', 'ep'), 'tp'), parts along dimension 0, may hold values from -48 to 48
- cache_latent: bfloat16 [64, 256, 512], P(('groups', 'ep')), parts along dimension 0, may hold values from -4 to 4
- cache_rope: bfloat16 [64, 64, 256], P(('groups', 'ep')), parts along dimension 0, may hold values from -4 to 4
- lengths: int32 [64], P(('groups', 'ep')), parts along dimension 0, may hold values from 16 to 256, as said below
Outputs:
- moe_out: bfloat16 [256, 3584], P(('groups', 'ep'), 'tp'), parts along dimension 0
- attn_latent: bfloat16 [64, 64, 512], P(('groups', 'ep'), 'tp'), parts along dimension 0
There are 2 independent parts, one for each index of `groups`. A program takes and returns all parts, laid end to end along the dimension named above; an argument that names none is the same for every part. Nothing has to cross between parts.
Inputs may be any that keep to these rules, and one draw needn't show every extreme that they name: `routes`: each row names 4 different experts; in each aligned block of 16 rows (the rows of one index of ep) no expert is named more than 16 times, and one expert, the same in every block, is named exactly 16 times in each block. `lengths`: one sequence has 256 live positions and one has 16.
All inputs are finite; a program needn't handle non-finite values.
Results may differ from a plain program's by a relative error of at most 0.0085.
Values may be sent and summed in bfloat16 or wider, within the bound.
A program may use at most 128 MiB of HBM per device.

v0:
```python
import jax
import jax.numpy as jnp
from jax import lax
from jax.sharding import PartitionSpec as P

softmax_scale = 192.0 ** (-0.5)
routed_scale = 2.5


def local(
    hidden,
    routes,
    router_weight,
    gate_weight,
    up_weight,
    down_weight,
    q_latent,
    q_rope,
    cache_latent,
    cache_rope,
    lengths,
):
    token_count, top_count = routes.shape
    expert_count = lax.axis_size("ep")
    capacity = min(token_count, 4 * token_count * top_count // expert_count)
    partial_logits = jnp.dot(hidden, router_weight, preferred_element_type=jnp.float32)
    logits = lax.psum(partial_logits, "tp")
    affinity = jax.nn.sigmoid(logits)
    expert_iota = jnp.arange(expert_count, dtype=jnp.int32)
    chosen_mask = routes[:, :, None] == expert_iota[None, None, :]
    chosen = jnp.sum(jnp.where(chosen_mask, affinity[:, None, :], 0.0), axis=2)
    gates = routed_scale * chosen / jnp.sum(chosen, axis=1, keepdims=True)
    flat_mask = chosen_mask.reshape(token_count * top_count, expert_count).astype(jnp.int32)
    earlier = jnp.cumsum(flat_mask, axis=0) - flat_mask
    within = jnp.sum(flat_mask * earlier, axis=1).reshape(token_count, top_count)
    slot_index = routes * capacity + within
    slot_iota = jnp.arange(expert_count * capacity, dtype=jnp.int32)
    placing = jnp.sum(
        (slot_index[None, :, :] == slot_iota[:, None, None]).astype(jnp.int32), axis=2
    )
    placing = placing.astype(jnp.bfloat16)
    outgoing = jnp.dot(placing, hidden, preferred_element_type=jnp.float32).astype(jnp.bfloat16)
    outgoing = outgoing.reshape(expert_count, capacity, hidden.shape[1])
    received = lax.all_to_all(outgoing, "ep", split_axis=0, concat_axis=0, tiled=True)
    received = lax.all_gather(received, "tp", axis=2, tiled=True)
    source_count, slot_count, feature_count = received.shape
    flat_rows = received.reshape(source_count * slot_count, feature_count)
    gate_part = jnp.dot(flat_rows, gate_weight[0], preferred_element_type=jnp.float32)
    up_part = jnp.dot(flat_rows, up_weight[0], preferred_element_type=jnp.float32)
    active = (jax.nn.silu(gate_part) * up_part).astype(jnp.bfloat16)
    partial_out = jnp.dot(active, down_weight[0], preferred_element_type=jnp.float32)
    summed = lax.psum_scatter(partial_out, "tp", scatter_dimension=1, tiled=True).astype(
        jnp.bfloat16
    )
    summed = summed.reshape(source_count, slot_count, summed.shape[1])
    returned = lax.all_to_all(summed, "ep", split_axis=0, concat_axis=0, tiled=True)
    scores = jnp.einsum("bhl,bjl->bhj", q_latent, cache_latent, preferred_element_type=jnp.float32)
    scores = scores + jnp.einsum(
        "bhr,brj->bhj", q_rope, cache_rope, preferred_element_type=jnp.float32
    )
    scores = scores * softmax_scale
    position = jnp.arange(cache_latent.shape[1], dtype=jnp.int32)
    live = position[None, None, :] < lengths[:, None, None]
    scores = jnp.where(live, scores, -jnp.inf)
    highest = jnp.max(scores, axis=2, keepdims=True)
    expo = jnp.where(live, jnp.exp(scores - highest), 0.0)
    attn_probs = (expo / jnp.sum(expo, axis=2, keepdims=True)).astype(jnp.bfloat16)
    attn_latent = jnp.einsum(
        "bhj,bjl->bhl", attn_probs, cache_latent, preferred_element_type=jnp.float32
    )
    attn_latent = attn_latent.astype(jnp.bfloat16)
    returned_flat = returned.reshape(expert_count * capacity, returned.shape[2])
    picked = jnp.take(returned_flat, slot_index.reshape(-1), axis=0).reshape(
        token_count, top_count, returned.shape[2]
    )
    moe_out = jnp.sum(gates[:, :, None] * picked.astype(jnp.float32), axis=1).astype(jnp.bfloat16)
    return (moe_out, attn_latent)


def solution(mesh):
    return jax.shard_map(
        local,
        mesh=mesh,
        in_specs=(
            P(("groups", "ep"), "tp"),
            P(("groups", "ep"), None),
            P("tp", None),
            P("ep", None, "tp"),
            P("ep", None, "tp"),
            P("ep", "tp", None),
            P(("groups", "ep"), "tp", None),
            P(("groups", "ep"), "tp", None),
            P(("groups", "ep"), None, None),
            P(("groups", "ep"), None, None),
            P(("groups", "ep")),
        ),
        out_specs=(P(("groups", "ep"), "tp"), P(("groups", "ep"), "tp", None)),
        check_vma=False,
    )
```

profile of v0, /device:TPU:0, one launch (start us, length us, event | category | flops | bytes accessed | tf_op | source)
XLA Modules:
  0.0 79.6 jit_solution(17327252212873637987)
XLA Ops:
  7.2 0.0 copy-start
  7.2 0.0 reduce-scatter.2.cloned.1.call-start
  7.2 0.8 %copy.22 = s32[16,4]{1,0:T(8,128)S(1)} copy(s32[16,4]{0,1:T(4,128)} %param.12) | data formatting | bytes 512 | tf_op args[1]
  8.1 0.1 eq.38
  8.2 0.1 fusion.27
  8.2 0.1 reduce_window_sum.11
  8.3 0.2 select_reduce_fusion
  8.5 0.1 reshape.109
  8.6 0.1 copy.24
  8.7 0.1 convert_reduce_fusion
  8.8 1.1 %convolution_convert_fusion = bf16[128,1792]{1,0:T(8,128)(2,1)S(1)} fusion(bf16[16,1792]{1,0:T(8,128)(2,1)} %param.11, s32[128,16]{0,1:T(8,128)S(1)} %convert_reduce_fusion), kind=kOutput, calls=%fused_computation.8 | convolution fusion | flops 7571456 | bytes 524288 | tf_op jit(solution)/shard_map/dot_general | solution.py:42
  9.9 20.3 %all_to_all.10 = bf16[8,16,1792]{2,1,0:T(8,128)(2,1)S(1)} all-to-all(bf16[8,16,1792]{2,1,0:T(8,128)(2,1)S(1)} %bitcast.36), channel_id=1, replica_groups=mesh['groups'=2,'ep'=8,'tp'=2] {'ep'}, dimensions={0} | all-to-all | bytes 917504 | tf_op jit(solution)/shard_map/all_to_all | solution.py:44
  30.2 2.5 %all_gather.3 = bf16[8,16,3584]{2,1,0:T(8,128)(2,1)S(1)} all-gather(bf16[8,16,1792]{2,1,0:T(8,128)(2,1)S(1)} %all_to_all.10), channel_id=1, replica_groups=mesh['groups'=2,'ep'=8,'tp'=2] {'tp'}, dimensions={2}, use_global_device_ids=true | all-gather | bytes 1376256 | tf_op jit(solution)/shard_map/all_gather | solution.py:45
  32.7 2.7 %fusion.5 = f32[128,512]{1,0:T(8,128)S(1)} fusion(bf16[128,3584]{1,0:T(8,128)(2,1)S(1)} %bitcast.34, bf16[1,3584,512]{2,1,0:T(8,128)(2,1)} %param.14), kind=kOutput, calls=%fused_computation.6 | convolution fusion | flops 469762048 | bytes 4849664 | tf_op jit(solution)/shard_map/dot_general | solution.py:48
  35.4 0.0 copy-start.1
  35.4 0.0 copy-start.5
  35.4 0.0 copy-start.6
  35.4 0.0 copy-start.2
  35.4 5.7 %fusion.1 = f32[128,3584]{1,0:T(8,128)} fusion(bf16[1,512,3584]{2,1,0:T(8,128)(2,1)} %param.16, bf16[128,3584]{1,0:T(8,128)(2,1)S(1)} %bitcast.35, bf16[1,3584,512]{2,1,0:T(8,128)(2,1)} %param.15, f32[128,512]{1,0:T(8,128)S(1)} %fusion.5), kind=kOutput, calls=%fused_computation.2 | convolution fusion | flops 939917312 | bytes 10354688 | tf_op jit(solution)/shard_map/dot_general | solution.py:51
  41.1 0.0 copy-start.7
  41.1 0.0 copy-start.3
  41.1 0.0 copy-start.4
  41.1 0.0 reduce-scatter.2.cloned.1.call-update
  41.1 0.1 reshape.114
  41.2 0.0 copy-done.1
  41.2 0.0 copy-done.5
  41.2 0.1 fusion.34
  41.3 2.5 %psum.7 = f32[16,8]{0,1:T(8,128)S(1)} all-reduce(f32[16,8]{0,1:T(8,128)S(1)} %fusion.34), channel_id=1, replica_groups=mesh['groups'=2,'ep'=8,'tp'=2] {'tp'}, use_global_device_ids=true, to_apply=%region_0.0 | all-reduce | flops 128 | bytes 1024 | tf_op jit(solution)/shard_map/psum | solution.py:27
  43.8 0.0 copy-done.6
  43.9 0.1 copy.21
  44.0 0.0 copy-done
  44.0 0.0 copy-done.2
  44.0 0.4 fusion.35
  44.4 5.2 %reduce-scatter.2.cloned.1.call-done = f32[128,1792]{1,0:T(8,128)} async-done(((f32[128,3584]{1,0:T(8,128)}), f32[128,1792]{1,0:T(8,128)}) %reduce-scatter.2.cloned.1.call-update) | async-done | bytes 917520 | tf_op jit(solution)/shard_map/reduce_scatter | solution.py:52
  49.6 2.0 %convert_element_type.35 = bf16[128,1792]{1,0:T(8,128)(2,1)} convert(f32[128,1792]{1,0:T(8,128)} %reduce-scatter.2.cloned.1.call-done) | non-fusion elementwise | flops 229376 | bytes 1376256 | tf_op jit(solution)/shard_map/convert_element_type | solution.py:52
  51.6 5.9 %all-to-all-start.1 = ((bf16[8,16,1792]{2,1,0:T(8,128)(2,1)}), bf16[8,16,1792]{2,1,0:T(8,128)(2,1)S(1)}, u32[]{:S(2)}, u32[]{:S(2)}) async-start(bf16[8,16,1792]{2,1,0:T(8,128)(2,1)} %bitcast.5), calls=%async_computation.2 | async-start | bytes 917504 | tf_op jit(solution)/shard_map/all_to_all | solution.py:56
  57.4 0.0 copy-done.7
  57.4 0.1 iota_compare_fusion.3
  57.5 0.0 copy-done.3
  57.5 0.0 copy-done.4
  57.5 0.2 fusion.17
  57.7 0.2 fusion.33
  57.9 1.0 %convolution_convert_fusion.1 = bf16[4,32,512]{2,1,0:T(8,128)(2,1)} fusion(bf16[4,256,512]{2,1,0:T(8,128)(2,1)S(1)} %copy-done, f32[4,32]{1,0:T(4,128)S(1)} %fusion.33, f32[4,32,256]{2,1,0:T(8,128)S(1)} %fusion.17, pred[4,256]{1,0:T(4,128)(4,1)S(1)} %iota_compare_fusion.3), kind=kOutput, calls=%fused_computation.11 | convolution fusion | flops 33751424 | bytes 1312256 | tf_op jit(solution)/shard_map/bhj,bjl->bhl/dot_general | solution.py:68
  58.8 12.0 %all-to-all-done.1 = bf16[8,16,1792]{2,1,0:T(8,128)(2,1)S(1)} async-done(((bf16[8,16,1792]{2,1,0:T(8,128)(2,1)}), bf16[8,16,1792]{2,1,0:T(8,128)(2,1)S(1)}, u32[]{:S(2)}, u32[]{:S(2)}) %all-to-all-start.1) | async-done | bytes 458784 | tf_op jit(solution)/shard_map/all_to_all | solution.py:56
  70.8 0.7 gather_fusion
  71.6 0.1 gather.7
  71.7 1.1 %multiply_reduce_fusion = bf16[16,1792]{1,0:T(8,128)(2,1)} fusion(bf16[16,4,1792]{2,1,0:T(4,128)(2,1)S(1)} %gather.7, f32[16,4]{1,0:T(8,128)S(1)} %copy.21, pred[16,4]{1,0:T(8,128)(4,1)S(1)} %get-tuple-element.4), kind=kLoop, calls=%fused_computation.18 | loop fusion | flops 430080 | bytes 287040 | tf_op jit(solution)/shard_map/reduce_sum | solution.py:76
  (6 shorter events, 0.1 us)
Async XLA Ops:
  7.2 36.8 %copy-start = (bf16[4,256,512]{2,1,0:T(8,128)(2,1)S(1)}, bf16[4,256,512]{2,1,0:T(8,128)(2,1)}, u32[]{:S(2)}) copy-start(bf16[4,256,512]{2,1,0:T(8,128)(2,1)} %param.19) | copy-start | bytes 3145732
  7.2 42.4 %reduce-scatter.2.cloned.1.call-start = ((), (), s32[]{:S(2)}) async-start(), calls=%async_computation.3 | async-start | bytes 2752512 | tf_op jit(solution)/shard_map/reduce_scatter | solution.py:52
  35.4 5.9 %copy-start.1 = (bf16[16,1792]{1,0:T(8,128)(2,1)S(1)}, bf16[16,1792]{1,0:T(8,128)(2,1)}, u32[]{:S(2)}) copy-start(bf16[16,1792]{1,0:T(8,128)(2,1)} %param.11) | copy-start | bytes 172036
  35.4 5.9 %copy-start.5 = (bf16[1792,8]{0,1:T(8,128)(2,1)S(1)}, bf16[1792,8]{0,1:T(8,128)(2,1)}, u32[]{:S(2)}) copy-start(bf16[1792,8]{0,1:T(8,128)(2,1)} %param.13) | copy-start | bytes 86020
  35.4 8.4 %copy-start.6 = (s32[16,4]{0,1:T(4,128)S(1)}, s32[16,4]{0,1:T(4,128)}, u32[]{:S(2)}) copy-start(s32[16,4]{0,1:T(4,128)} %param.12) | copy-start | bytes 772
  35.4 8.6 %copy-start.2 = (bf16[4,32,512]{2,1,0:T(8,128)(2,1)S(1)}, bf16[4,32,512]{2,1,0:T(8,128)(2,1)}, u32[]{:S(2)}) copy-start(bf16[4,32,512]{2,1,0:T(8,128)(2,1)} %param.17) | copy-start | bytes 393220
  41.1 16.3 %copy-start.7 = (s32[4]{0:T(128)S(1)}, s32[4]{0:T(128)}, u32[]{:S(2)}) copy-start(s32[4]{0:T(128)} %param.21) | copy-start | bytes 52
  41.1 16.4 %copy-start.3 = (bf16[4,64,256]{2,1,0:T(8,128)(2,1)S(1)}, bf16[4,64,256]{2,1,0:T(8,128)(2,1)}, u32[]{:S(2)}) copy-start(bf16[4,64,256]{2,1,0:T(8,128)(2,1)} %param.20) | copy-start | bytes 393220
  41.1 16.4 %copy-start.4 = (bf16[4,32,64]{2,1,0:T(8,128)(2,1)S(1)}, bf16[4,32,64]{2,1,0:T(8,128)(2,1)}, u32[]{:S(2)}) copy-start(bf16[4,32,64]{2,1,0:T(8,128)(2,1)} %param.18) | copy-start | bytes 49156
  51.6 19.3 %all-to-all-start.1 = ((bf16[8,16,1792]{2,1,0:T(8,128)(2,1)}), bf16[8,16,1792]{2,1,0:T(8,128)(2,1)S(1)}, u32[]{:S(2)}, u32[]{:S(2)}) async-start(bf16[8,16,1792]{2,1,0:T(8,128)(2,1)} %bitcast.5), calls=%async_computation.2 | async-start | bytes 917504 | tf_op jit(solution)/shard_map/all_to_all | solution.py:56
Sparse Core Ops, SparseCore 0:
  41.2 8.2 reduce-scatter.1
where the time goes:
time: 80 us; the launch traced here: 79.6 us
  blocking collectives  25.2 us (32%)
  waiting for transfers between devices  17.2 us (22%)
  between operations  14.2 us (18%)
  matrix products  11.2 us (14%)
  starting transfers between devices  5.91 us (7%)
  other arithmetic  3.88 us (5%)
  local copies, waits for them, and re-layouts  2.09 us (3%)
    all_to_all x1, blocking collectives, local(): lax.all_to_all(outgoing, 'ep', split_axis=0, concat_axis=0, tiled=True)  20.3 us
    all_to_all x1, waiting for transfers between devices, local(): lax.all_to_all(summed, 'ep', split_axis=0, concat_axis=0, tiled=True)  12 us
    all_to_all x1, starting transfers between devices, local(): lax.all_to_all(summed, 'ep', split_axis=0, concat_axis=0, tiled=True)  5.87 us
    dot_general x1, matrix products, local(): jnp.dot(active, down_weight[0], preferred_element_type=jnp.float32)  5.69 us
    reduce_scatter x1, waiting for transfers between devices, local(): lax.psum_scatter(partial_out, 'tp', scatter_dimension=1, tiled=True)  5.18 us
    dot_general x1, matrix products, local(): jnp.dot(flat_rows, gate_weight[0], preferred_element_type=jnp.float32)  2.68 us
    psum x1, blocking collectives, local(): logits = lax.psum(partial_logits, 'tp')  2.46 us
    all_gather x1, blocking collectives, local(): received = lax.all_gather(received, 'tp', axis=2, tiled=True)  2.45 us
  transfers between devices with their start and end apart: 2, of which 2 were waited for; matrix products, arithmetic and copies ran while one was open for 3% of the time, Pallas kernels for 0%

commit v1 on v0

--- a/solution.py
+++ b/solution.py
@@ -1,3 +1,4 @@
+import functools
 import jax
 import jax.numpy as jnp
 from jax import lax
@@ -5,6 +6,13 @@
 
 softmax_scale = 192.0 ** (-0.5)
 routed_scale = 2.5
+
+
+def sheets_launch(sample, device_axis):
+    return lax.all_gather(sample, axis_name=device_axis).sum(axis=0)
+
+
+runs_cover = functools.partial(sheets_launch, device_axis="tp")
 
 
 def local(
@@ -24,7 +32,7 @@
     expert_count = lax.axis_size("ep")
     capacity = min(token_count, 4 * token_count * top_count // expert_count)
     partial_logits = jnp.dot(hidden, router_weight, preferred_element_type=jnp.float32)
-    logits = lax.psum(partial_logits, "tp")
+    logits = runs_cover(partial_logits)
     affinity = jax.nn.sigmoid(logits)
     expert_iota = jnp.arange(expert_count, dtype=jnp.int32)
     chosen_mask = routes[:, :, None] == expert_iota[None, None, :]

time: 80 us -> 80 us (level)
    psum x1 -> x0, blocking collectives: 2.46 us -> none  [local(): logits = lax.psum(partial_logits, 'tp')]
    all_gather x0 -> x1, blocking collectives: none -> 1.82 us  [sheets_launch(): return lax.all_gather(sample, axis_name=device_axis).sum(axis=0)]
where the time goes in v1:
time: 80 us; the launch traced here: 79.6 us
  blocking collectives  24.6 us (31%)
  waiting for transfers between devices  17.8 us (22%)
  between operations  14.2 us (18%)
  matrix products  11.2 us (14%)
  starting transfers between devices  5.91 us (7%)
  other arithmetic  3.88 us (5%)
  local copies, waits for them, and re-layouts  2.09 us (3%)
    all_to_all x1, blocking collectives, local(): lax.all_to_all(outgoing, 'ep', split_axis=0, concat_axis=0, tiled=True)  20.3 us
    all_to_all x1, waiting for transfers between devices, local(): lax.all_to_all(summed, 'ep', split_axis=0, concat_axis=0, tiled=True)  12 us
    all_to_all x1, starting transfers between devices, local(): lax.all_to_all(summed, 'ep', split_axis=0, concat_axis=0, tiled=True)  5.87 us
    reduce_scatter x1, waiting for transfers between devices, local(): lax.psum_scatter(partial_out, 'tp', scatter_dimension=1, tiled=True)  5.81 us
    dot_general x1, matrix products, local(): jnp.dot(active, down_weight[0], preferred_element_type=jnp.float32)  5.69 us
    dot_general x1, matrix products, local(): jnp.dot(flat_rows, gate_weight[0], preferred_element_type=jnp.float32)  2.68 us
    all_gather x1, blocking collectives, local(): received = lax.all_gather(received, 'tp', axis=2, tiled=True)  2.45 us
    convert_element_type x1, other arithmetic, local(): lax.psum_scatter(partial_out, 'tp', scatter_dimension=1, tiled=True)  2 us
  transfers between devices with their start and end apart: 2, of which 2 were waited for; matrix products, arithmetic and copies ran while one was open for 3% of the time, Pallas kernels for 0%

profile of v1, /device:TPU:0, one launch (start us, length us, event | category | flops | bytes accessed | tf_op | source)
XLA Modules:
  0.0 79.6 jit_solution(11592886174548873208)
XLA Ops:
  7.2 0.0 copy-start
  7.2 0.0 reduce-scatter.2.cloned.1.call-start
  7.2 0.8 %copy.24 = s32[16,4]{1,0:T(8,128)S(1)} copy(s32[16,4]{0,1:T(4,128)} %param.12) | data formatting | bytes 512 | tf_op args[1]
  8.1 0.1 eq.38
  8.2 0.1 fusion.27
  8.2 0.1 reduce_window_sum.11
  8.3 0.2 select_reduce_fusion
  8.5 0.1 reshape.114
  8.6 0.1 copy.26
  8.7 0.1 convert_reduce_fusion
  8.8 1.1 %convolution_convert_fusion = bf16[128,1792]{1,0:T(8,128)(2,1)S(1)} fusion(bf16[16,1792]{1,0:T(8,128)(2,1)} %param.11, s32[128,16]{0,1:T(8,128)S(1)} %convert_reduce_fusion), kind=kOutput, calls=%fused_computation.8 | convolution fusion | flops 7571456 | bytes 524288 | tf_op jit(solution)/shard_map/dot_general | solution.py:50
  9.9 20.3 %all_to_all.10 = bf16[8,16,1792]{2,1,0:T(8,128)(2,1)S(1)} all-to-all(bf16[8,16,1792]{2,1,0:T(8,128)(2,1)S(1)} %bitcast.38), channel_id=1, replica_groups=mesh['groups'=2,'ep'=8,'tp'=2] {'ep'}, dimensions={0} | all-to-all | bytes 917504 | tf_op jit(solution)/shard_map/all_to_all | solution.py:52
  30.2 2.5 %all_gather.11 = bf16[8,16,3584]{2,1,0:T(8,128)(2,1)S(1)} all-gather(bf16[8,16,1792]{2,1,0:T(8,128)(2,1)S(1)} %all_to_all.10), channel_id=1, replica_groups=mesh['groups'=2,'ep'=8,'tp'=2] {'tp'}, dimensions={2}, use_global_device_ids=true | all-gather | bytes 1376256 | tf_op jit(solution)/shard_map/all_gather | solution.py:53
  32.7 2.7 %fusion.5 = f32[128,512]{1,0:T(8,128)S(1)} fusion(bf16[128,3584]{1,0:T(8,128)(2,1)S(1)} %bitcast.36, bf16[1,3584,512]{2,1,0:T(8,128)(2,1)} %param.14), kind=kOutput, calls=%fused_computation.6 | convolution fusion | flops 469762048 | bytes 4849664 | tf_op jit(solution)/shard_map/dot_general | solution.py:56
  35.4 0.0 copy-start.1
  35.4 0.0 copy-start.5
  35.4 0.0 copy-start.6
  35.4 0.0 copy-start.2
  35.4 5.7 %fusion.1 = f32[128,3584]{1,0:T(8,128)} fusion(bf16[1,512,3584]{2,1,0:T(8,128)(2,1)} %param.16, bf16[128,3584]{1,0:T(8,128)(2,1)S(1)} %bitcast.37, bf16[1,3584,512]{2,1,0:T(8,128)(2,1)} %param.15, f32[128,512]{1,0:T(8,128)S(1)} %fusion.5), kind=kOutput, calls=%fused_computation.2 | convolution fusion | flops 939917312 | bytes 10354688 | tf_op jit(solution)/shard_map/dot_general | solution.py:59
  41.1 0.0 copy-start.7
  41.1 0.0 copy-start.3
  41.1 0.0 copy-start.4
  41.1 0.0 reduce-scatter.2.cloned.1.call-update
  41.1 0.1 reshape.119
  41.2 0.0 copy-done.1
  41.2 0.0 copy-done.5
  41.2 0.1 convolution_bitcast_fusion
  41.3 1.8 %all-gather.1 = f32[2,16,8]{1,2,0:T(8,128)S(1)} all-gather(f32[1,16,8]{1,2,0:T(8,128)S(1)} %convolution_bitcast_fusion), channel_id=2, replica_groups=mesh['groups'=2,'ep'=8,'tp'=2] {'tp'}, dimensions={0}, use_global_device_ids=true | all-gather | bytes 1536 | tf_op jit(solution)/shard_map/all_gather | solution.py:12
  43.2 0.0 copy-done.6
  43.2 0.1 copy.23
  43.3 0.0 copy-done
  43.3 0.0 copy-done.2
  43.3 0.4 fusion.34
  43.8 5.8 %reduce-scatter.2.cloned.1.call-done = f32[128,1792]{1,0:T(8,128)} async-done(((f32[128,3584]{1,0:T(8,128)}), f32[128,1792]{1,0:T(8,128)}) %reduce-scatter.2.cloned.1.call-update) | async-done | bytes 917520 | tf_op jit(solution)/shard_map/reduce_scatter | solution.py:60
  49.6 2.0 %convert_element_type.35 = bf16[128,1792]{1,0:T(8,128)(2,1)} convert(f32[128,1792]{1,0:T(8,128)} %reduce-scatter.2.cloned.1.call-done) | non-fusion elementwise | flops 229376 | bytes 1376256 | tf_op jit(solution)/shard_map/convert_element_type | solution.py:60
  51.6 5.9 %all-to-all-start.1 = ((bf16[8,16,1792]{2,1,0:T(8,128)(2,1)}), bf16[8,16,1792]{2,1,0:T(8,128)(2,1)S(1)}, u32[]{:S(2)}, u32[]{:S(2)}) async-start(bf16[8,16,1792]{2,1,0:T(8,128)(2,1)} %bitcast.6), calls=%async_computation.2 | async-start | bytes 917504 | tf_op jit(solution)/shard_map/all_to_all | solution.py:64
  57.4 0.0 copy-done.7
  57.4 0.1 iota_compare_fusion.3
  57.5 0.0 copy-done.3
  57.5 0.0 copy-done.4
  57.5 0.2 fusion.17
  57.7 0.2 fusion.33
  57.9 1.0 %convolution_convert_fusion.1 = bf16[4,32,512]{2,1,0:T(8,128)(2,1)} fusion(bf16[4,256,512]{2,1,0:T(8,128)(2,1)S(1)} %copy-done, f32[4,32]{1,0:T(4,128)S(1)} %fusion.33, f32[4,32,256]{2,1,0:T(8,128)S(1)} %fusion.17, pred[4,256]{1,0:T(4,128)(4,1)S(1)} %iota_compare_fusion.3), kind=kOutput, calls=%fused_computation.11 | convolution fusion | flops 33751424 | bytes 1312256 | tf_op jit(solution)/shard_map/bhj,bjl->bhl/dot_general | solution.py:76
  58.8 12.0 %all-to-all-done.1 = bf16[8,16,1792]{2,1,0:T(8,128)(2,1)S(1)} async-done(((bf16[8,16,1792]{2,1,0:T(8,128)(2,1)}), bf16[8,16,1792]{2,1,0:T(8,128)(2,1)S(1)}, u32[]{:S(2)}, u32[]{:S(2)}) %all-to-all-start.1) | async-done | bytes 458784 | tf_op jit(solution)/shard_map/all_to_all | solution.py:64
  70.8 0.7 gather_fusion
  71.6 0.1 gather.7
  71.7 1.1 %multiply_reduce_fusion = bf16[16,1792]{1,0:T(8,128)(2,1)} fusion(bf16[16,4,1792]{2,1,0:T(4,128)(2,1)S(1)} %gather.7, f32[16,4]{1,0:T(8,128)S(1)} %copy.23, pred[16,4]{1,0:T(8,128)(4,1)S(1)} %get-tuple-element.4), kind=kLoop, calls=%fused_computation.19 | loop fusion | flops 430080 | bytes 287040 | tf_op jit(solution)/shard_map/reduce_sum | solution.py:84
  (7 shorter events, 0.1 us)
Async XLA Ops:
  7.2 36.2 %copy-start = (bf16[4,256,512]{2,1,0:T(8,128)(2,1)S(1)}, bf16[4,256,512]{2,1,0:T(8,128)(2,1)}, u32[]{:S(2)}) copy-start(bf16[4,256,512]{2,1,0:T(8,128)(2,1)} %param.19) | copy-start | bytes 3145732
  7.2 42.4 %reduce-scatter.2.cloned.1.call-start = ((), (), s32[]{:S(2)}) async-start(), calls=%async_computation.3 | async-start | bytes 2752512 | tf_op jit(solution)/shard_map/reduce_scatter | solution.py:60
  35.4 5.9 %copy-start.1 = (bf16[16,1792]{1,0:T(8,128)(2,1)S(1)}, bf16[16,1792]{1,0:T(8,128)(2,1)}, u32[]{:S(2)}) copy-start(bf16[16,1792]{1,0:T(8,128)(2,1)} %param.11) | copy-start | bytes 172036
  35.4 5.9 %copy-start.5 = (bf16[1792,8]{0,1:T(8,128)(2,1)S(1)}, bf16[1792,8]{0,1:T(8,128)(2,1)}, u32[]{:S(2)}) copy-start(bf16[1792,8]{0,1:T(8,128)(2,1)} %param.13) | copy-start | bytes 86020
  35.4 7.8 %copy-start.6 = (s32[16,4]{0,1:T(4,128)S(1)}, s32[16,4]{0,1:T(4,128)}, u32[]{:S(2)}) copy-start(s32[16,4]{0,1:T(4,128)} %param.12) | copy-start | bytes 772
  35.4 8.0 %copy-start.2 = (bf16[4,32,512]{2,1,0:T(8,128)(2,1)S(1)}, bf16[4,32,512]{2,1,0:T(8,128)(2,1)}, u32[]{:S(2)}) copy-start(bf16[4,32,512]{2,1,0:T(8,128)(2,1)} %param.17) | copy-start | bytes 393220
  41.1 16.3 %copy-start.7 = (s32[4]{0:T(128)S(1)}, s32[4]{0:T(128)}, u32[]{:S(2)}) copy-start(s32[4]{0:T(128)} %param.21) | copy-start | bytes 52
  41.1 16.4 %copy-start.3 = (bf16[4,64,256]{2,1,0:T(8,128)(2,1)S(1)}, bf16[4,64,256]{2,1,0:T(8,128)(2,1)}, u32[]{:S(2)}) copy-start(bf16[4,64,256]{2,1,0:T(8,128)(2,1)} %param.20) | copy-start | bytes 393220
  41.1 16.4 %copy-start.4 = (bf16[4,32,64]{2,1,0:T(8,128)(2,1)S(1)}, bf16[4,32,64]{2,1,0:T(8,128)(2,1)}, u32[]{:S(2)}) copy-start(bf16[4,32,64]{2,1,0:T(8,128)(2,1)} %param.18) | copy-start | bytes 49156
  51.6 19.3 %all-to-all-start.1 = ((bf16[8,16,1792]{2,1,0:T(8,128)(2,1)}), bf16[8,16,1792]{2,1,0:T(8,128)(2,1)S(1)}, u32[]{:S(2)}, u32[]{:S(2)}) async-start(bf16[8,16,1792]{2,1,0:T(8,128)(2,1)} %bitcast.6), calls=%async_computation.2 | async-start | bytes 917504 | tf_op jit(solution)/shard_map/all_to_all | solution.py:64
Sparse Core Ops, SparseCore 0:
  41.2 8.2 reduce-scatter.1
